TPU v7x, 256 devices: a whole 4x4x8 slice. The times are simulated.
256 devices in a mesh: expert: 8 (over y, core), shard: 32 (over z, x).
Axes of the slice: x: 4, y: 4, z: 8, core: 2. Of those that a mesh axis runs over, the one named last changes fastest.
Arguments:
- master_gate: float32 [128, 2048, 768], P('expert', 'shard'), may hold values from -0.125 to 0.125
- second_gate: bfloat16 [128, 2048, 768], P('expert', 'shard'), may hold values from -0.0625 to 0.0625
- master_up: float32 [128, 2048, 768], P('expert', 'shard'), may hold values from -0.125 to 0.125
- second_up: bfloat16 [128, 2048, 768], P('expert', 'shard'), may hold values from -0.0625 to 0.0625
- router_weight: float32 [2048, 128], P('shard', 'expert'), may hold values from -0.125 to 0.125
- router_gain: float32 [2048], P('shard'), may hold values from 0.25 to 1.75
Outputs:
- final_gate: bfloat16 [128, 768, 2048], P('expert', 'shard')
- final_up: bfloat16 [128, 768, 2048], P('expert', 'shard')
- serve_router: bfloat16 [2048, 128], replicated
All inputs are finite; a program needn't handle non-finite values.
Results may differ from a plain program's by a relative error of at most 0.001.
Values may be sent and summed in bfloat16 or wider, within the bound.
A program may use at most 64 MiB of HBM per device.

v0:
```python
import jax
import jax.numpy as jnp
from jax import lax
from jax.sharding import Mesh
from jax.sharding import PartitionSpec as P

EXPERT = ("expert_0", "expert_1")


def laid_out(parts, dim):
    shape = list(parts.shape[1:])
    shape[dim] *= parts.shape[0]
    return jnp.moveaxis(parts, 0, dim).reshape(shape)


def copy_for_each(x, axis):
    copies = jnp.broadcast_to(x, (lax.axis_size(axis), *x.shape))
    return lax.all_to_all(copies, axis, split_axis=0, concat_axis=0, tiled=True)


def gathered_copies(x, axis, dim):
    return laid_out(copy_for_each(x, axis), dim)


def edges_of(length, count):
    turn = length // count
    if turn >= 8:
        turn -= turn % 8
    return [turn * k for k in range(1, count)]


def gather_in_order(x, axes, turns):
    parts = x
    for k in turns:
        parts = lax.all_gather(parts, axes[k])
    done = turns[::-1]
    back = [done.index(k) for k in range(len(axes))]
    parts = parts.transpose(*back, *range(len(axes), parts.ndim))
    return parts.reshape(-1, *x.shape)


def gather_all_axes(x, axes, dim):
    numbers = list(range(len(axes)))[::-1]
    cut = x.shape.index(max(x.shape[:-1] or x.shape))
    edges = [0, *edges_of(x.shape[cut], len(axes)), x.shape[cut]]
    gathered = []
    for k, (start, end) in enumerate(zip(edges, edges[1:])):
        if end > start:
            section = lax.slice_in_dim(x, start, end, axis=cut)
            gathered.append(gather_in_order(section, axes, numbers[k:] + numbers[:k]))
    return laid_out(jnp.concatenate(gathered, axis=cut + 1), dim)


def shards(master_gate, second_gate, master_up, second_up, router_weight, router_gain):
    merged_gate = master_gate + second_gate.astype(jnp.float32)
    merged_up = master_up + second_up.astype(jnp.float32)
    narrow_gate, narrow_up = (merged_gate.astype(jnp.bfloat16), merged_up.astype(jnp.bfloat16))
    final_gate, final_up = (
        lax.all_to_all(narrow_gate, "shard", split_axis=2, concat_axis=1, tiled=True),
        lax.all_to_all(narrow_up, "shard", split_axis=2, concat_axis=1, tiled=True),
    )
    final_gate = jnp.transpose(final_gate, (0, 2, 1))
    final_up = jnp.transpose(final_up, (0, 2, 1))
    part_router = (router_weight * router_gain[:, None]).astype(jnp.bfloat16)
    row_router = gathered_copies(part_router, "shard", 0)
    serve_router = gather_all_axes(row_router, EXPERT, 1)
    return (final_gate, final_up, serve_router)


def solution(mesh):
    split = Mesh(mesh.devices.reshape(4, 2, mesh.shape["shard"]), ("expert_0", "expert_1", "shard"))
    in_specs = (
        P(EXPERT, "shard", None),
        P(EXPERT, "shard", None),
        P(EXPERT, "shard", None),
        P(EXPERT, "shard", None),
        P("shard", EXPERT),
        P("shard"),
    )
    out_specs = (P(EXPERT, "shard", None), P(EXPERT, "shard", None), P())
    return jax.shard_map(
        shards, mesh=split, in_specs=in_specs, out_specs=out_specs, check_vma=False
    )
```

profile of v0, /device:TPU:6, one launch (start us, length us, event | category | flops | bytes accessed | tf_op | source)
XLA Modules:
  0.0 138.5 jit_solution(3208780866263310215)
XLA Ops:
  0.6 0.7 multiply_convert_fusion
  1.4 0.8 reshape.31
  2.1 11.6 %all-to-all-start.2 = ((bf16[32,2,512]{2,1,0:T(2,128)(2,1)}), bf16[32,2,512]{2,1,0:T(2,128)(2,1)S(1)}, u32[]{:S(2)}, u32[]{:S(2)}) async-start(bf16[32,2,512]{2,1,0:T(2,128)(2,1)} %reshape.31), calls=%async_computation.2 | async-start | bytes 131072 | tf_op jit(solution)/shard_map/all_to_all | solution.py:18
  13.7 3.9 %add_convert_fusion.1 = bf16[16,64,768]{2,1,0:T(8,128)(2,1)} fusion(f32[16,64,768]{2,1,0:T(8,128)} %param.6, bf16[16,64,768]{2,1,0:T(8,128)(2,1)} %param.7), kind=kLoop, calls=%fused_computation.1 | loop fusion | flops 2359296 | bytes 6291456 | tf_op jit(solution)/shard_map/convert_element_type | solution.py:57
  17.6 4.0 %copy.48 = bf16[16,64,768]{1,0,2:T(8,128)(2,1)S(1)} copy(bf16[16,64,768]{2,1,0:T(8,128)(2,1)} %add_convert_fusion.1) | data formatting | bytes 3145728 | tf_op jit(solution)/shard_map/convert_element_type | solution.py:57
  21.6 3.2 %reshape.27 = bf16[32,2,12288]{2,1,0:T(2,128)(2,1)} reshape(bf16[768,16,64]{2,1,0:T(8,128)(2,1)S(1)} %bitcast.34) | data formatting | bytes 3145728
  24.8 10.1 %all-to-all-start = ((bf16[32,2,12288]{2,1,0:T(2,128)(2,1)}), bf16[32,2,12288]{2,1,0:T(2,128)(2,1)}, u32[]{:S(2)}, u32[]{:S(2)}) async-start(bf16[32,2,12288]{2,1,0:T(2,128)(2,1)} %reshape.27), calls=%async_computation | async-start | bytes 3145728 | tf_op jit(solution)/shard_map/all_to_all | solution.py:59
  34.9 3.0 %add_convert_fusion = bf16[16,64,768]{2,1,0:T(8,128)(2,1)} fusion(f32[16,64,768]{2,1,0:T(8,128)S(1)} %copy-done, bf16[16,64,768]{2,1,0:T(8,128)(2,1)} %param.9), kind=kLoop, calls=%fused_computation | loop fusion | flops 2359296 | bytes 6291456 | tf_op jit(solution)/shard_map/convert_element_type | solution.py:57
  37.9 4.0 %copy.51 = bf16[16,64,768]{1,0,2:T(8,128)(2,1)S(1)} copy(bf16[16,64,768]{2,1,0:T(8,128)(2,1)} %add_convert_fusion) | data formatting | bytes 3145728 | tf_op jit(solution)/shard_map/convert_element_type | solution.py:57
  41.9 3.2 %reshape.29 = bf16[32,2,12288]{2,1,0:T(2,128)(2,1)} reshape(bf16[768,16,64]{2,1,0:T(8,128)(2,1)S(1)} %bitcast.35) | data formatting | bytes 3145728
  45.1 28.6 %all-to-all-done = bf16[32,2,12288]{2,1,0:T(2,128)(2,1)} async-done(((bf16[32,2,12288]{2,1,0:T(2,128)(2,1)}), bf16[32,2,12288]{2,1,0:T(2,128)(2,1)}, u32[]{:S(2)}, u32[]{:S(2)}) %all-to-all-start) | async-done | bytes 1572896 | tf_op jit(solution)/shard_map/all_to_all | solution.py:59
  73.7 5.6 %all-to-all-start.1 = ((bf16[32,2,12288]{2,1,0:T(2,128)(2,1)}), bf16[32,2,12288]{2,1,0:T(2,128)(2,1)}, u32[]{:S(2)}, u32[]{:S(2)}) async-start(bf16[32,2,12288]{2,1,0:T(2,128)(2,1)} %reshape.29), calls=%async_computation.1 | async-start | bytes 3145728 | tf_op jit(solution)/shard_map/all_to_all | solution.py:60
  79.3 0.1 reshape.32
  79.6 12.7 %all_gather.29 = bf16[4,1024,16]{1,2,0:T(8,128)(2,1)S(1)} all-gather(bf16[1,1024,16]{1,2,0:T(8,128)(2,1)S(1)} %all_gather.28), channel_id=1, replica_groups=mesh['expert_0'=4,'expert_1'=2,'shard'=32] {'expert_0'}, dimensions={0}, use_global_device_ids=true | all-gather | bytes 163840 | tf_op jit(solution)/shard_map/all_gather | solution.py:35
  92.3 2.0 %all-gather.1 = bf16[8,1024,16]{1,2,0:T(8,128)(2,1)S(1)} all-gather(bf16[4,1024,16]{1,2,0:T(8,128)(2,1)S(1)} %all_gather.29), channel_id=3, replica_groups=mesh['expert_0'=4,'expert_1'=2,'shard'=32] {'expert_1'}, dimensions={0}, use_global_device_ids=true | all-gather | bytes 393216 | tf_op jit(solution)/shard_map/all_gather | solution.py:35
  94.5 1.9 %all_gather.25 = bf16[2,1024,16]{1,2,0:T(8,128)(2,1)S(1)} all-gather(bf16[1,1024,16]{1,2,0:T(8,128)(2,1)S(1)} %all_gather.24), channel_id=1, replica_groups=mesh['expert_0'=4,'expert_1'=2,'shard'=32] {'expert_1'}, dimensions={0}, use_global_device_ids=true | all-gather | bytes 98304 | tf_op jit(solution)/shard_map/all_gather | solution.py:35
  96.3 12.4 %all-gather = bf16[8,1024,16]{1,2,0:T(8,128)(2,1)S(1)} all-gather(bf16[2,1024,16]{1,2,0:T(8,128)(2,1)S(1)} %all_gather.25), channel_id=2, replica_groups=mesh['expert_0'=4,'expert_1'=2,'shard'=32] {'expert_0'}, dimensions={0}, use_global_device_ids=true | all-gather | bytes 327680 | tf_op jit(solution)/shard_map/all_gather | solution.py:35
  108.8 1.0 copy.57
  109.8 5.1 %reshape.28 = bf16[768,16,64]{2,1,0:T(8,128)(2,1)S(1)} reshape(bf16[32,2,12288]{2,1,0:T(2,128)(2,1)} %all-to-all-done) | data formatting | bytes 3145728
  114.9 3.7 %copy.50 = bf16[16,32,64,24]{2,1,3,0:T(8,128)(2,1)} copy(bf16[16,32,64,24]{2,0,3,1:T(8,128)(2,1)S(1)} %bitcast.36) | data formatting | bytes 3145728 | tf_op jit(solution)/shard_map/all_to_all | solution.py:59
  118.6 5.6 %all_to_all.32 = bf16[16,2048,24]{1,2,0:T(8,128)(2,1)} reshape(bf16[16,32,64,24]{2,1,3,0:T(8,128)(2,1)} %copy.50) | data formatting | bytes 3145728 | tf_op jit(solution)/shard_map/all_to_all | solution.py:59
  124.1 5.1 %reshape.30 = bf16[768,16,64]{2,1,0:T(8,128)(2,1)S(1)} reshape(bf16[32,2,12288]{2,1,0:T(2,128)(2,1)} %all-to-all-done.1) | data formatting | bytes 3145728
  129.2 3.7 %copy.53 = bf16[16,32,64,24]{2,1,3,0:T(8,128)(2,1)} copy(bf16[16,32,64,24]{2,0,3,1:T(8,128)(2,1)S(1)} %bitcast.37) | data formatting | bytes 3145728 | tf_op jit(solution)/shard_map/all_to_all | solution.py:60
  132.9 5.6 %all_to_all.36 = bf16[16,2048,24]{1,2,0:T(8,128)(2,1)} reshape(bf16[16,32,64,24]{2,1,3,0:T(8,128)(2,1)} %copy.53) | data formatting | bytes 3145728 | tf_op jit(solution)/shard_map/all_to_all | solution.py:60
  (12 shorter events, 0.4 us)
Async XLA Ops:
  2.1 22.7 %all-to-all-start.2 = ((bf16[32,2,512]{2,1,0:T(2,128)(2,1)}), bf16[32,2,512]{2,1,0:T(2,128)(2,1)S(1)}, u32[]{:S(2)}, u32[]{:S(2)}) async-start(bf16[32,2,512]{2,1,0:T(2,128)(2,1)} %reshape.31), calls=%async_computation.2 | async-start | bytes 131072 | tf_op jit(solution)/shard_map/all_to_all | solution.py:18
  24.8 10.1 %copy-start = (f32[16,64,768]{2,1,0:T(8,128)S(1)}, f32[16,64,768]{2,1,0:T(8,128)}, u32[]{:S(2)}) copy-start(f32[16,64,768]{2,1,0:T(8,128)} %param.8) | copy-start | bytes 9437188
  24.8 48.9 %all-to-all-start = ((bf16[32,2,12288]{2,1,0:T(2,128)(2,1)}), bf16[32,2,12288]{2,1,0:T(2,128)(2,1)}, u32[]{:S(2)}, u32[]{:S(2)}) async-start(bf16[32,2,12288]{2,1,0:T(2,128)(2,1)} %reshape.27), calls=%async_computation | async-start | bytes 3145728 | tf_op jit(solution)/shard_map/all_to_all | solution.py:59
  73.7 50.4 %all-to-all-start.1 = ((bf16[32,2,12288]{2,1,0:T(2,128)(2,1)}), bf16[32,2,12288]{2,1,0:T(2,128)(2,1)}, u32[]{:S(2)}, u32[]{:S(2)}) async-start(bf16[32,2,12288]{2,1,0:T(2,128)(2,1)} %reshape.29), calls=%async_computation.1 | async-start | bytes 3145728 | tf_op jit(solution)/shard_map/all_to_all | solution.py:60
where the time goes:
time: 139 us; the launch traced here: 138 us
  local copies, waits for them, and re-layouts  45.3 us (33%)
  blocking collectives  28.9 us (21%)
  waiting for transfers between devices  28.6 us (21%)
  starting transfers between devices  27.3 us (20%)
  other arithmetic  7.6 us (5%)
    all_gather x4, blocking collectives, gather_in_order(): parts = lax.all_gather(parts, axes[k])  28.9 us
    all_to_all x1, waiting for transfers between devices, shards(): lax.all_to_all(narrow_gate, 'shard', split_axis=2, concat_axis=1, tiled=T...  28.6 us
    unnamed x10, local copies, waits for them, and re-layouts  18.5 us
    all_to_all x1, starting transfers between devices, copy_for_each(): return lax.all_to_all(copies, axis, split_axis=0, concat_axis=0, tiled=True)  11.6 us
    all_to_all x1, starting transfers between devices, shards(): lax.all_to_all(narrow_gate, 'shard', split_axis=2, concat_axis=1, tiled=T...  10.1 us
    all_to_all x2, local copies, waits for them, and re-layouts, shards(): lax.all_to_all(narrow_gate, 'shard', split_axis=2, concat_axis=1, tiled=T...  9.25 us
    all_to_all x2, local copies, waits for them, and re-layouts, shards(): lax.all_to_all(narrow_up, 'shard', split_axis=2, concat_axis=1, tiled=True)  9.25 us
    all_to_all x1, starting transfers between devices, shards(): lax.all_to_all(narrow_up, 'shard', split_axis=2, concat_axis=1, tiled=True)  5.61 us
  transfers between devices with their start and end apart: 3, of which 1 were waited for; matrix products, arithmetic and copies ran while one was open for 23% of the time, Pallas kernels for 0%

commit v1 on v0

v1 whole, which is shorter than its diff:
```python
import jax
import jax.numpy as jnp
from jax import lax
from jax.experimental import pallas as pl
from jax.experimental.pallas import tpu as pltpu
from jax.sharding import PartitionSpec as P

MESH = pl.DeviceIdType.MESH
NZ, NX = 8, 4
NS = NZ * NX
NE = 8
E = 16
PAIRS = E // 2
ROWS = 64
COLS = 768
TAKE = COLS // NS
BLOCK = 2 * TAKE
F32, BF16 = jnp.float32, jnp.bfloat16


def exchange(
    mg, sg, mu, su, rw, rg,
    gate, up, router,
    mg_v, sg_v, mu_v, su_v, rw_v, rg_v, wide, send, recv, ra, rb, rc,
    load_sem, small_sem, send_sem, recv_sem, a_send, a_recv, b_send, b_recv, c_send, c_recv,
):
    shard, expert = lax.axis_index("shard"), lax.axis_index("expert")
    z, x = shard // NX, shard % NX

    def plane(step):
        return lax.rem(z + step // NX, NZ) * NX + lax.rem(x + lax.rem(step, NX), NX)

    def loads(p):
        at = pl.ds(2 * p, 2)
        return [
            pltpu.make_async_copy(src.at[at], dst.at[at], load_sem.at[k, p])
            for k, (src, dst) in enumerate(((mg, mg_v), (sg, sg_v), (mu, mu_v), (su, su_v)))
        ]

    for copy in loads(0):
        copy.start()
    small = (
        pltpu.make_async_copy(rw, rw_v, small_sem.at[0]),
        pltpu.make_async_copy(rg, rg_v, small_sem.at[1]),
    )
    for copy in small:
        copy.start()

    barrier = pltpu.get_barrier_semaphore()

    @pl.loop(1, NS)
    def _(step):
        pl.semaphore_signal(barrier, 1, device_id={"shard": plane(step)}, device_id_type=MESH)

    @pl.loop(1, NE)
    def _(step):
        to = lax.rem(expert + step, NE)
        pl.semaphore_signal(barrier, 1, device_id={"expert": to}, device_id_type=MESH)

    for copy in loads(1):
        copy.start()

    for copy in small:
        copy.wait()
    wide[...] = jnp.zeros((128, 128), F32)
    wide[0:16, 0:ROWS] = (rw_v[...] * rg_v[...]).astype(BF16).astype(F32)
    tall = wide[...].T
    packed = tall[0:8]
    for k in range(1, 8):
        packed = packed + pltpu.roll(tall[8 * k : 8 * k + 8], 16 * k, 1)
    ra[z] = packed

    def a_copy(step):
        to = lax.rem(z + step, NZ) * NX + x
        return pltpu.make_async_remote_copy(
            ra.at[z], ra.at[z], a_send, a_recv, device_id={"shard": to}, device_id_type=MESH
        )

    def b_copy(step):
        to = z * NX + lax.rem(x + step, NX)
        return pltpu.make_async_remote_copy(
            rb.at[x], rb.at[x], b_send, b_recv, device_id={"shard": to}, device_id_type=MESH
        )

    def c_copy(step):
        to = lax.rem(expert + step, NE)
        return pltpu.make_async_remote_copy(
            rb, rc.at[expert], c_send, c_recv, device_id={"expert": to}, device_id_type=MESH
        )

    def block_copy(p, step):
        to = plane(step)
        return pltpu.make_async_remote_copy(
            send.at[p, to],
            recv.at[p, shard],
            send_sem.at[p],
            recv_sem.at[p],
            device_id={"shard": to},
            device_id_type=MESH,
        )

    def took(ref, sem):
        pltpu.make_async_copy(ref, ref, sem).wait()

    @pl.loop(0, PAIRS)
    def _(p):
        for copy in loads(p):
            copy.wait()

        @pl.when(p + 2 < PAIRS)
        def _():
            for copy in loads(p + 2):
                copy.start()

        turned = []
        for i in range(2):
            e = 2 * p + i
            a = jnp.concatenate(
                [mg_v[e] + sg_v[e].astype(F32), mu_v[e] + su_v[e].astype(F32)], axis=0
            )
            turned.append(a.T.reshape(NS, TAKE, 128))
        send[p] = jnp.concatenate(turned, axis=1).astype(BF16)
        recv[p, shard] = send[p, shard]

        @pl.when(p == 0)
        def _():
            pl.semaphore_wait(barrier, NS - 1 + NE - 1)

            @pl.loop(1, NZ)
            def _(step):
                a_copy(step).start()

        @pl.when(p == 2)
        def _():
            took(ra.at[pl.ds(0, NZ - 1)], a_recv)
            rb[x] = ra[...].reshape(8 * NZ, 128).astype(BF16)

            @pl.loop(1, NX)
            def _(step):
                b_copy(step).start()

        @pl.when(p == 4)
        def _():
            took(rb.at[pl.ds(0, NX - 1)], b_recv)
            rc[expert] = rb[...]

            @pl.loop(1, NE)
            def _(step):
                c_copy(step).start()

        @pl.loop(1, NS)
        def _(step):
            block_copy(p, step).start()

    def merge(p):
        took(recv.at[p, pl.ds(0, NS - 1)], recv_sem.at[p])
        low = lax.broadcasted_iota(jnp.int32, (BLOCK, 128), 1) < 64
        for j in range(NS // 2):
            a, b = recv[p, 2 * j].astype(F32), recv[p, 2 * j + 1].astype(F32)
            g = jnp.where(low, a, pltpu.roll(b, 64, 1))
            u = jnp.where(low, pltpu.roll(a, 64, 1), b)
            for i in range(2):
                rows = slice(TAKE * i, TAKE * (i + 1))
                gate[2 * p + i, :, 128 * j : 128 * (j + 1)] = g[rows].astype(BF16)
                up[2 * p + i, :, 128 * j : 128 * (j + 1)] = u[rows].astype(BF16)

    @pl.loop(0, PAIRS // 2)
    def _(p):
        merge(p)

    took(rc.at[pl.ds(0, NE - 1)], c_recv)
    lane = lax.broadcasted_iota(jnp.int32, (8, 128), 1) // 16

    @pl.loop(0, NX)
    def _(i):
        @pl.loop(0, NZ // 2)
        def _(h):
            total = [[None] * 8, [None] * 8]
            for e in range(NE):
                both = rc[e, i, pl.ds(pl.multiple_of(16 * h, 16), 16), :].astype(F32)
                for q in range(2):
                    one = both[8 * q : 8 * q + 8]
                    for k in range(8):
                        turn = 16 * ((e - k) % 8)
                        moved = pltpu.roll(one, turn, 1) if turn else one
                        old = total[q][k]
                        total[q][k] = moved if old is None else jnp.where(lane == e, moved, old)
            for q in range(2):
                row = pl.multiple_of(((2 * h + q) * NX + i) * ROWS, ROWS)
                router[pl.ds(row, ROWS), :] = jnp.concatenate(total[q], axis=0).astype(BF16)

    @pl.loop(PAIRS // 2, PAIRS)
    def _(p):
        merge(p)

    @pl.loop(0, PAIRS)
    def _(p):
        took(send.at[p, pl.ds(0, NS - 1)], send_sem.at[p])

    took(ra.at[pl.ds(0, NZ - 1)], a_send)
    took(rb.at[pl.ds(0, NX - 1)], b_send)
    took(rc.at[pl.ds(0, NE - 1)], c_send)


def store(gate, up, router, gate_out, up_out, router_out, sem):
    copies = [
        pltpu.make_async_copy(src, dst, sem.at[k])
        for k, (src, dst) in enumerate(((gate, gate_out), (up, up_out), (router, router_out)))
    ]
    for copy in copies:
        copy.start()
    for copy in copies:
        copy.wait()


def shards(master_gate, second_gate, master_up, second_up, router_weight, router_gain):
    dma = pltpu.SemaphoreType.DMA
    hbm, vmem = pl.BlockSpec(memory_space=pltpu.HBM), pl.BlockSpec(memory_space=pltpu.VMEM)
    shapes = (
        jax.ShapeDtypeStruct((E, TAKE, NS * ROWS), BF16),
        jax.ShapeDtypeStruct((E, TAKE, NS * ROWS), BF16),
        jax.ShapeDtypeStruct((NS * ROWS, 16 * NE), BF16),
    )
    held = pl.pallas_call(
        exchange,
        out_shape=shapes,
        in_specs=[hbm] * 6,
        out_specs=(vmem,) * 3,
        scratch_shapes=[
            pltpu.VMEM((E, ROWS, COLS), F32),
            pltpu.VMEM((E, ROWS, COLS), BF16),
            pltpu.VMEM((E, ROWS, COLS), F32),
            pltpu.VMEM((E, ROWS, COLS), BF16),
            pltpu.VMEM((16, ROWS), F32),
            pltpu.VMEM((1, ROWS), F32),
            pltpu.VMEM((128, 128), F32),
            pltpu.VMEM((PAIRS, NS, BLOCK, 128), BF16),
            pltpu.VMEM((PAIRS, NS, BLOCK, 128), BF16),
            pltpu.VMEM((NZ, 8, 128), F32),
            pltpu.VMEM((NX, 8 * NZ, 128), BF16),
            pltpu.VMEM((NE, NX, 8 * NZ, 128), BF16),
            dma((4, PAIRS)),
            dma((2,)),
            dma((PAIRS,)),
            dma((PAIRS,)),
        ]
        + [dma] * 6,
        compiler_params=pltpu.CompilerParams(
            collective_id=0, has_side_effects=True, vmem_limit_bytes=30 << 20
        ),
        name="exchange",
    )(
        *(
            pltpu.with_memory_space_constraint(a, pltpu.HBM)
            for a in (
                master_gate, second_gate, master_up, second_up,
                router_weight.T, router_gain.reshape(1, ROWS),
            )
        )
    )
    return pl.pallas_call(
        store,
        out_shape=shapes,
        in_specs=[vmem] * 3,
        out_specs=(hbm,) * 3,
        scratch_shapes=[dma((3,))],
        compiler_params=pltpu.CompilerParams(vmem_limit_bytes=8 << 20),
        name="store",
    )(*held)


def solution(mesh):
    in_specs = (P("expert", "shard", None),) * 4 + (P("shard", "expert"), P("shard"))
    out_specs = (P("expert", "shard", None), P("expert", "shard", None), P())
    return jax.shard_map(shards, mesh=mesh, in_specs=in_specs, out_specs=out_specs, check_vma=False)
```

time: 139 us -> 84.3 us (0.61)
  Pallas kernels: 0 us -> 82.3 us
  local copies, waits for them, and re-layouts: 45.3 us -> 0 us
  blocking collectives: 28.9 us -> 0 us
  waiting for transfers between devices: 28.6 us -> 0 us
  starting transfers between devices: 27.3 us -> 0 us
  other arithmetic: 7.6 us -> 0 us
    pallas_call x0 -> x2, Pallas kernels: none -> 82.3 us  [the longest x1 80.5 us: shards(): pl.pallas_call(exchange, out_shape=shapes, in_specs=[hbm] * 6, out_specs=...]
    all_gather x4 -> x0, blocking collectives: 28.9 us -> none  [gather_in_order(): parts = lax.all_gather(parts, axes[k])]
    all_to_all x3 -> x0, waiting for transfers between devices: 28.6 us -> none  [the longest x1 28.6 us: shards(): lax.all_to_all(narrow_gate, 'shard', split_axis=2, concat_axis=1, tiled=T...]
    all_to_all x3 -> x0, starting transfers between devices: 27.3 us -> none  [the longest x1 11.6 us: copy_for_each(): return lax.all_to_all(copies, axis, split_axis=0, concat_axis=0, tiled=True)]
    all_to_all x4 -> x0, local copies, waits for them, and re-layouts: 18.5 us -> none  [the longest x2 9.25 us: shards(): lax.all_to_all(narrow_gate, 'shard', split_axis=2, concat_axis=1, tiled=T...]
    unnamed x10 -> x0, local copies, waits for them, and re-layouts: 18.5 us -> none
    convert_element_type x2 -> x0, local copies, waits for them, and re-layouts: 8.03 us -> none  [the longest x1 4.02 us: shards(): merged_gate.astype(jnp.bfloat16)]
    convert_element_type x3 -> x0, other arithmetic: 7.55 us -> none  [the longest x1 3.9 us: shards(): merged_gate.astype(jnp.bfloat16)]
  transfers between devices with their start and end apart: 3 -> 0, of which waited for: 1 -> 0; matrix products, arithmetic and copies ran while one was open for 23% -> 0% of each run, Pallas kernels for 0% -> 0%
where the time goes in v1:
time: 84.3 us; the launch traced here: 83 us
  Pallas kernels  82.3 us (98%)
    pallas_call x1, Pallas kernels, shards(): pl.pallas_call(exchange, out_shape=shapes, in_specs=[hbm] * 6, out_specs=...  80.5 us
    pallas_call x1, Pallas kernels, shards(): pl.pallas_call(store, out_shape=shapes, in_specs=[vmem] * 3, out_specs=(h...  1.86 us

profile of v1, /device:TPU:6, one launch (start us, length us, event | category | flops | bytes accessed | tf_op | source)
XLA Modules:
  0.0 83.0 jit_solution(5758272110861287560)
XLA Ops:
  0.6 80.5 %exchange.1 = (bf16[16,24,2048]{2,1,0:T(8,128)(2,1)S(1)}, bf16[16,24,2048]{2,1,0:T(8,128)(2,1)S(1)}, bf16[2048,128]{1,0:T(8,128)(2,1)S(1)}) custom-call(f32[16,64,768]{2,1,0:T(8,128)} %mg.1, bf16[16,64,768]{2,1,0:T(8,128)(2,1)} %sg.1, f32[16,64,768]{2,1,0:T(8,128)} %mu.1, bf16[16,64,768]{2,1,0:T(8,128)(2,1)} %su.1, f32[16,64]{1,0:T(8,128)} %bitcast.2, ...), custom_call_target="tpu_custom_call" | custom-call | tf_op jit(solution)/shard_map/exchange/pallas_call | solution.py:224
  81.1 1.9 %store.1 = (bf16[16,24,2048]{2,1,0:T(8,128)(2,1)}, bf16[16,24,2048]{2,1,0:T(8,128)(2,1)}, bf16[2048,128]{1,0:T(8,128)(2,1)}) custom-call(bf16[16,24,2048]{2,1,0:T(8,128)(2,1)S(1)} %get-tuple-element.6.gate, bf16[16,24,2048]{2,1,0:T(8,128)(2,1)S(1)} %get-tuple-element.7.up, bf16[2048,128]{1,0:T(8,128)(2,1)S(1)} %get-tuple-element.8.router), custom_call_target="tpu_custom_call" | custom-call | tf_op jit(solution)/shard_map/store/pallas_call | solution.py:261

commit v2 on v1

--- a/solution.py
+++ b/solution.py
@@ -16,6 +16,8 @@
 TAKE = COLS // NS
 BLOCK = 2 * TAKE
 F32, BF16 = jnp.float32, jnp.bfloat16
+OFFSETS = [(dz, dx) for dz in (4, 3, 5, 2, 6, 1, 7, 0) for dx in (2, 1, 3, 0) if dz or dx]
+PIECES = 1
 
 
 def exchange(
@@ -26,9 +28,9 @@
 ):
     shard, expert = lax.axis_index("shard"), lax.axis_index("expert")
     z, x = shard // NX, shard % NX
-
-    def plane(step):
-        return lax.rem(z + step // NX, NZ) * NX + lax.rem(x + lax.rem(step, NX), NX)
+    row = [lax.rem(z + k, NZ) * NX for k in range(NZ)]
+    column = [lax.rem(x + k, NX) for k in range(NX)]
+    other = [lax.rem(expert + k, NE) for k in range(NE)]
 
     def loads(p):
         at = pl.ds(2 * p, 2)
@@ -48,14 +50,11 @@
 
     barrier = pltpu.get_barrier_semaphore()
 
-    @pl.loop(1, NS)
-    def _(step):
-        pl.semaphore_signal(barrier, 1, device_id={"shard": plane(step)}, device_id_type=MESH)
-
-    @pl.loop(1, NE)
-    def _(step):
-        to = lax.rem(expert + step, NE)
-        pl.semaphore_signal(barrier, 1, device_id={"expert": to}, device_id_type=MESH)
+    for dz, dx in OFFSETS:
+        to = row[dz] + column[dx]
+        pl.semaphore_signal(barrier, 1, device_id={"shard": to}, device_id_type=MESH)
+    for k in range(1, NE):
+        pl.semaphore_signal(barrier, 1, device_id={"expert": other[k]}, device_id_type=MESH)
 
     for copy in loads(1):
         copy.start()
@@ -68,28 +67,28 @@
     packed = tall[0:8]
     for k in range(1, 8):
         packed = packed + pltpu.roll(tall[8 * k : 8 * k + 8], 16 * k, 1)
-    ra[z] = packed
+    ra[z] = packed.astype(BF16)
 
     def a_copy(step):
-        to = lax.rem(z + step, NZ) * NX + x
+        to = row[step] + x
         return pltpu.make_async_remote_copy(
             ra.at[z], ra.at[z], a_send, a_recv, device_id={"shard": to}, device_id_type=MESH
         )
 
     def b_copy(step):
-        to = z * NX + lax.rem(x + step, NX)
+        to = row[0] + column[step]
         return pltpu.make_async_remote_copy(
             rb.at[x], rb.at[x], b_send, b_recv, device_id={"shard": to}, device_id_type=MESH
         )
 
     def c_copy(step):
-        to = lax.rem(expert + step, NE)
+        to = other[step]
         return pltpu.make_async_remote_copy(
             rb, rc.at[expert], c_send, c_recv, device_id={"expert": to}, device_id_type=MESH
         )
 
-    def block_copy(p, step):
-        to = plane(step)
+    def block_copy(p, dz, dx):
+        to = row[dz] + column[dx]
         return pltpu.make_async_remote_copy(
             send.at[p, to],
             recv.at[p, shard],
@@ -126,17 +125,15 @@
         def _():
             pl.semaphore_wait(barrier, NS - 1 + NE - 1)
 
-            @pl.loop(1, NZ)
-            def _(step):
+            for step in range(1, NZ):
                 a_copy(step).start()
 
         @pl.when(p == 2)
         def _():
             took(ra.at[pl.ds(0, NZ - 1)], a_recv)
-            rb[x] = ra[...].reshape(8 * NZ, 128).astype(BF16)
-
-            @pl.loop(1, NX)
-            def _(step):
+            rb[x] = ra[...].astype(F32).reshape(8 * NZ, 128).astype(BF16)
+
+            for step in range(1, NX):
                 b_copy(step).start()
 
         @pl.when(p == 4)
@@ -144,13 +141,11 @@
             took(rb.at[pl.ds(0, NX - 1)], b_recv)
             rc[expert] = rb[...]
 
-            @pl.loop(1, NE)
-            def _(step):
+            for step in range(1, NE):
                 c_copy(step).start()
 
-        @pl.loop(1, NS)
-        def _(step):
-            block_copy(p, step).start()
+        for dz, dx in OFFSETS:
+            block_copy(p, dz, dx).start()
 
     def merge(p):
         took(recv.at[p, pl.ds(0, NS - 1)], recv_sem.at[p])
@@ -203,10 +198,12 @@
 
 
 def store(gate, up, router, gate_out, up_out, router_out, sem):
-    copies = [
-        pltpu.make_async_copy(src, dst, sem.at[k])
-        for k, (src, dst) in enumerate(((gate, gate_out), (up, up_out), (router, router_out)))
-    ]
+    copies = []
+    for src, dst in ((gate, gate_out), (up, up_out), (router, router_out)):
+        size = src.shape[0] // PIECES
+        for k in range(PIECES):
+            at = pl.ds(size * k, size)
+            copies.append(pltpu.make_async_copy(src.at[at], dst.at[at], sem.at[len(copies)]))
     for copy in copies:
         copy.start()
     for copy in copies:
@@ -236,7 +233,7 @@
             pltpu.VMEM((128, 128), F32),
             pltpu.VMEM((PAIRS, NS, BLOCK, 128), BF16),
             pltpu.VMEM((PAIRS, NS, BLOCK, 128), BF16),
-            pltpu.VMEM((NZ, 8, 128), F32),
+            pltpu.VMEM((NZ, 8, 128), BF16),
             pltpu.VMEM((NX, 8 * NZ, 128), BF16),
             pltpu.VMEM((NE, NX, 8 * NZ, 128), BF16),
             dma((4, PAIRS)),
@@ -263,7 +260,7 @@
         out_shape=shapes,
         in_specs=[vmem] * 3,
         out_specs=(hbm,) * 3,
-        scratch_shapes=[dma((3,))],
+        scratch_shapes=[dma((3 * PIECES,))],
         compiler_params=pltpu.CompilerParams(vmem_limit_bytes=8 << 20),
         name="store",
     )(*held)

time: 84.3 us -> 83.3 us (0.988)
  Pallas kernels: 82.3 us -> 81.4 us
    pallas_call x1, Pallas kernels: 80.5 us -> 79.6 us  [shards(): pl.pallas_call(exchange, out_shape=shapes, in_specs=[hbm] * 6, out_specs=...]
where the time goes in v2:
time: 83.3 us; the launch traced here: 82.1 us
  Pallas kernels  81.4 us (98%)
    pallas_call x1, Pallas kernels, shards(): pl.pallas_call(exchange, out_shape=shapes, in_specs=[hbm] * 6, out_specs=...  79.6 us
    pallas_call x1, Pallas kernels, shards(): pl.pallas_call(store, out_shape=shapes, in_specs=[vmem] * 3, out_specs=(h...  1.86 us

profile of v2, /device:TPU:6, one launch (start us, length us, event | category | flops | bytes accessed | tf_op | source)
XLA Modules:
  0.0 82.1 jit_solution(8463153682335094732)
XLA Ops:
  0.6 79.6 %exchange.1 = (bf16[16,24,2048]{2,1,0:T(8,128)(2,1)S(1)}, bf16[16,24,2048]{2,1,0:T(8,128)(2,1)S(1)}, bf16[2048,128]{1,0:T(8,128)(2,1)S(1)}) custom-call(f32[16,64,768]{2,1,0:T(8,128)} %mg.1, bf16[16,64,768]{2,1,0:T(8,128)(2,1)} %sg.1, f32[16,64,768]{2,1,0:T(8,128)} %mu.1, bf16[16,64,768]{2,1,0:T(8,128)(2,1)} %su.1, f32[16,64]{1,0:T(8,128)} %bitcast.2, ...), custom_call_target="tpu_custom_call" | custom-call | tf_op jit(solution)/shard_map/exchange/pallas_call | solution.py:221
  80.2 1.9 %store.1 = (bf16[16,24,2048]{2,1,0:T(8,128)(2,1)}, bf16[16,24,2048]{2,1,0:T(8,128)(2,1)}, bf16[2048,128]{1,0:T(8,128)(2,1)}) custom-call(bf16[16,24,2048]{2,1,0:T(8,128)(2,1)S(1)} %get-tuple-element.6.gate, bf16[16,24,2048]{2,1,0:T(8,128)(2,1)S(1)} %get-tuple-element.7.up, bf16[2048,128]{1,0:T(8,128)(2,1)S(1)} %get-tuple-element.8.router), custom_call_target="tpu_custom_call" | custom-call | tf_op jit(solution)/shard_map/store/pallas_call | solution.py:258

commit v3 on v2

--- a/solution.py
+++ b/solution.py
@@ -16,15 +16,28 @@
 TAKE = COLS // NS
 BLOCK = 2 * TAKE
 F32, BF16 = jnp.float32, jnp.bfloat16
-OFFSETS = [(dz, dx) for dz in (4, 3, 5, 2, 6, 1, 7, 0) for dx in (2, 1, 3, 0) if dz or dx]
-PIECES = 1
+NEAR = [(dz, dx) for dz in (1, 7, 0) for dx in (2, 1, 3, 0) if dz or dx]
+FAR = [(dz, dx) for dz in (4, 3, 5, 2, 6) for dx in (2, 1, 3, 0)]
+MID = 1
+
+
+def merged(blocks, gate, up):
+    low = lax.broadcasted_iota(jnp.int32, (BLOCK, 128), 1) < 64
+    for j in range(NS // 2):
+        a, b = blocks[2 * j].astype(F32), blocks[2 * j + 1].astype(F32)
+        g = jnp.where(low, a, pltpu.roll(b, 64, 1))
+        u = jnp.where(low, pltpu.roll(a, 64, 1), b)
+        for i in range(2):
+            rows = slice(TAKE * i, TAKE * (i + 1))
+            gate[i, :, 128 * j : 128 * (j + 1)] = g[rows].astype(BF16)
+            up[i, :, 128 * j : 128 * (j + 1)] = u[rows].astype(BF16)
 
 
 def exchange(
     mg, sg, mu, su, rw, rg,
-    gate, up, router,
-    mg_v, sg_v, mu_v, su_v, rw_v, rg_v, wide, send, recv, ra, rb, rc,
-    load_sem, small_sem, send_sem, recv_sem, a_send, a_recv, b_send, b_recv, c_send, c_recv,
+    gate, up, router, recv,
+    mg_v, sg_v, mu_v, su_v, rw_v, rg_v, wide, send, ra, rb, rc,
+    load_sem, small_sem, send_sem, recv_sem, near_sem, mid_sem, open_sem, all_sem, a_send, a_recv, b_send, b_recv, c_send, c_recv,
 ):
     shard, expert = lax.axis_index("shard"), lax.axis_index("expert")
     z, x = shard // NX, shard % NX
@@ -50,24 +63,17 @@
 
     barrier = pltpu.get_barrier_semaphore()
 
-    for dz, dx in OFFSETS:
+    for dz, dx in NEAR:
         to = row[dz] + column[dx]
         pl.semaphore_signal(barrier, 1, device_id={"shard": to}, device_id_type=MESH)
-    for k in range(1, NE):
-        pl.semaphore_signal(barrier, 1, device_id={"expert": other[k]}, device_id_type=MESH)
+
+    @pl.when(shard == 0)
+    def _():
+        for k in range(1, NE):
+            pl.semaphore_signal(barrier, 1, device_id={"expert": other[k]}, device_id_type=MESH)
 
     for copy in loads(1):
         copy.start()
-
-    for copy in small:
-        copy.wait()
-    wide[...] = jnp.zeros((128, 128), F32)
-    wide[0:16, 0:ROWS] = (rw_v[...] * rg_v[...]).astype(BF16).astype(F32)
-    tall = wide[...].T
-    packed = tall[0:8]
-    for k in range(1, 8):
-        packed = packed + pltpu.roll(tall[8 * k : 8 * k + 8], 16 * k, 1)
-    ra[z] = packed.astype(BF16)
 
     def a_copy(step):
         to = row[step] + x
@@ -98,6 +104,10 @@
             device_id_type=MESH,
         )
 
+    def tell(sem, step):
+        for dz in (step, NZ - step):
+            pl.semaphore_signal(sem, 1, device_id={"shard": row[dz] + x}, device_id_type=MESH)
+
     def took(ref, sem):
         pltpu.make_async_copy(ref, ref, sem).wait()
 
@@ -123,41 +133,72 @@
 
         @pl.when(p == 0)
         def _():
-            pl.semaphore_wait(barrier, NS - 1 + NE - 1)
-
-            for step in range(1, NZ):
-                a_copy(step).start()
-
-        @pl.when(p == 2)
+            pl.semaphore_wait(barrier, len(NEAR) + jnp.where(shard == 0, NE - 1, 0))
+            tell(near_sem, 1)
+
+        for dz, dx in NEAR:
+            block_copy(p, dz, dx).start()
+
+        @pl.when(p == 0)
+        def _():
+            for copy in small:
+                copy.wait()
+            wide[...] = jnp.zeros((128, 128), F32)
+            wide[0:16, 0:ROWS] = (rw_v[...] * rg_v[...]).astype(BF16).astype(F32)
+            tall = wide[...].T
+            packed = tall[0:8]
+            for k in range(1, 8):
+                packed = packed + pltpu.roll(tall[8 * k : 8 * k + 8], 16 * k, 1)
+            ra[z] = packed.astype(BF16)
+
+        @pl.when(p == MID)
+        def _():
+            pl.semaphore_wait(near_sem, 2)
+            tell(mid_sem, 2)
+
+    pl.semaphore_wait(mid_sem, 2)
+
+    @pl.when(shard == 0)
+    def _():
+        for k in range(1, NE):
+            pl.semaphore_signal(open_sem, 1, device_id={"expert": other[k]}, device_id_type=MESH)
+
+    for step in range(1, NZ):
+        a_copy(step).start()
+
+    @pl.loop(0, PAIRS)
+    def _(p):
+        for dz, dx in FAR:
+            block_copy(p, dz, dx).start()
+
+        @pl.when(p == 1)
         def _():
             took(ra.at[pl.ds(0, NZ - 1)], a_recv)
             rb[x] = ra[...].astype(F32).reshape(8 * NZ, 128).astype(BF16)
-
             for step in range(1, NX):
                 b_copy(step).start()
 
-        @pl.when(p == 4)
+        @pl.when((p == 2) & (shard == 0))
+        def _():
+            pl.semaphore_wait(open_sem, NE - 1)
+            for dz, dx in NEAR + FAR:
+                to = row[dz] + column[dx]
+                pl.semaphore_signal(all_sem, 1, device_id={"shard": to}, device_id_type=MESH)
+
+        @pl.when((p == 3) & (shard != 0))
+        def _():
+            pl.semaphore_wait(all_sem, 1)
+
+        @pl.when(p == 3)
         def _():
             took(rb.at[pl.ds(0, NX - 1)], b_recv)
             rc[expert] = rb[...]
-
             for step in range(1, NE):
                 c_copy(step).start()
 
-        for dz, dx in OFFSETS:
-            block_copy(p, dz, dx).start()
-
     def merge(p):
         took(recv.at[p, pl.ds(0, NS - 1)], recv_sem.at[p])
-        low = lax.broadcasted_iota(jnp.int32, (BLOCK, 128), 1) < 64
-        for j in range(NS // 2):
-            a, b = recv[p, 2 * j].astype(F32), recv[p, 2 * j + 1].astype(F32)
-            g = jnp.where(low, a, pltpu.roll(b, 64, 1))
-            u = jnp.where(low, pltpu.roll(a, 64, 1), b)
-            for i in range(2):
-                rows = slice(TAKE * i, TAKE * (i + 1))
-                gate[2 * p + i, :, 128 * j : 128 * (j + 1)] = g[rows].astype(BF16)
-                up[2 * p + i, :, 128 * j : 128 * (j + 1)] = u[rows].astype(BF16)
+        merged(recv.at[p], gate.at[pl.ds(2 * p, 2)], up.at[pl.ds(2 * p, 2)])
 
     @pl.loop(0, PAIRS // 2)
     def _(p):
@@ -184,9 +225,11 @@
                 row = pl.multiple_of(((2 * h + q) * NX + i) * ROWS, ROWS)
                 router[pl.ds(row, ROWS), :] = jnp.concatenate(total[q], axis=0).astype(BF16)
 
-    @pl.loop(PAIRS // 2, PAIRS)
+    @pl.loop(PAIRS // 2, PAIRS - 1)
     def _(p):
         merge(p)
+
+    took(recv.at[PAIRS - 1, pl.ds(0, NS - 1)], recv_sem.at[PAIRS - 1])
 
     @pl.loop(0, PAIRS)
     def _(p):
@@ -197,14 +240,24 @@
     took(rc.at[pl.ds(0, NE - 1)], c_send)
 
 
-def store(gate, up, router, gate_out, up_out, router_out, sem):
-    copies = []
-    for src, dst in ((gate, gate_out), (up, up_out), (router, router_out)):
-        size = src.shape[0] // PIECES
-        for k in range(PIECES):
-            at = pl.ds(size * k, size)
-            copies.append(pltpu.make_async_copy(src.at[at], dst.at[at], sem.at[len(copies)]))
-    for copy in copies:
+def store(gate, up, router, recv, gate_out, up_out, router_out, gate_v, up_v, sem):
+    first, last = pl.ds(0, E - 2), pl.ds(E - 2, 2)
+    copies = [
+        pltpu.make_async_copy(src, dst, sem.at[k])
+        for k, (src, dst) in enumerate(
+            (
+                (gate, gate_out.at[first]),
+                (up, up_out.at[first]),
+                (router, router_out),
+                (gate_v, gate_out.at[last]),
+                (up_v, up_out.at[last]),
+            )
+        )
+    ]
+    for copy in copies[:3]:
+        copy.start()
+    merged(recv.at[PAIRS - 1], gate_v, up_v)
+    for copy in copies[3:]:
         copy.start()
     for copy in copies:
         copy.wait()
@@ -218,11 +271,13 @@
         jax.ShapeDtypeStruct((E, TAKE, NS * ROWS), BF16),
         jax.ShapeDtypeStruct((NS * ROWS, 16 * NE), BF16),
     )
+    part = jax.ShapeDtypeStruct((E - 2, TAKE, NS * ROWS), BF16)
+    blocks = jax.ShapeDtypeStruct((PAIRS, NS, BLOCK, 128), BF16)
     held = pl.pallas_call(
         exchange,
-        out_shape=shapes,
+        out_shape=(part, part, shapes[2], blocks),
         in_specs=[hbm] * 6,
-        out_specs=(vmem,) * 3,
+        out_specs=(vmem,) * 4,
         scratch_shapes=[
             pltpu.VMEM((E, ROWS, COLS), F32),
             pltpu.VMEM((E, ROWS, COLS), BF16),
@@ -232,7 +287,6 @@
             pltpu.VMEM((1, ROWS), F32),
             pltpu.VMEM((128, 128), F32),
             pltpu.VMEM((PAIRS, NS, BLOCK, 128), BF16),
-            pltpu.VMEM((PAIRS, NS, BLOCK, 128), BF16),
             pltpu.VMEM((NZ, 8, 128), BF16),
             pltpu.VMEM((NX, 8 * NZ, 128), BF16),
             pltpu.VMEM((NE, NX, 8 * NZ, 128), BF16),
@@ -241,6 +295,7 @@
             dma((PAIRS,)),
             dma((PAIRS,)),
         ]
+        + [pltpu.SemaphoreType.REGULAR] * 4
         + [dma] * 6,
         compiler_params=pltpu.CompilerParams(
             collective_id=0, has_side_effects=True, vmem_limit_bytes=30 << 20
@@ -258,9 +313,9 @@
     return pl.pallas_call(
         store,
         out_shape=shapes,
-        in_specs=[vmem] * 3,
+        in_specs=[vmem] * 4,
         out_specs=(hbm,) * 3,
-        scratch_shapes=[dma((3 * PIECES,))],
+        scratch_shapes=[pltpu.VMEM((2, TAKE, NS * ROWS), BF16)] * 2 + [dma((5,))],
         compiler_params=pltpu.CompilerParams(vmem_limit_bytes=8 << 20),
         name="store",
     )(*held)

time: 83.3 us -> 81.7 us (0.981)
  Pallas kernels: 81.4 us -> 80.4 us
    pallas_call x2, Pallas kernels: 81.4 us -> 80.4 us  [the longest x1 78.5 us: shards(): pl.pallas_call(exchange, out_shape=(part, part, shapes[2], blocks), in_sp...]
where the time goes in v3:
time: 81.7 us; the launch traced here: 81 us
  Pallas kernels  80.4 us (98%)
    pallas_call x1, Pallas kernels, shards(): pl.pallas_call(exchange, out_shape=(part, part, shapes[2], blocks), in_sp...  78.5 us
    pallas_call x1, Pallas kernels, shards(): pl.pallas_call(store, out_shape=shapes, in_specs=[vmem] * 4, out_specs=(h...  1.87 us

profile of v3, /device:TPU:6, one launch (start us, length us, event | category | flops | bytes accessed | tf_op | source)
XLA Modules:
  0.0 81.0 jit_solution(2849477035744672647)
XLA Ops:
  0.6 78.5 %exchange.1 = (bf16[14,24,2048]{2,1,0:T(8,128)(2,1)S(1)}, bf16[14,24,2048]{2,1,0:T(8,128)(2,1)S(1)}, bf16[2048,128]{1,0:T(8,128)(2,1)S(1)}, bf16[8,32,48,128]{3,2,1,0:T(8,128)(2,1)S(1)}) custom-call(f32[16,64,768]{2,1,0:T(8,128)} %mg.1, bf16[16,64,768]{2,1,0:T(8,128)(2,1)} %sg.1, f32[16,64,768]{2,1,0:T(8,128)} %mu.1, bf16[16,64,768]{2,1,0:T(8,128)(2,1)} %su.1, ...), custom_call_target="tpu_custom_call" | custom-call | tf_op jit(solution)/shard_map/exchange/pallas_call | solution.py:276
  79.2 1.9 %store.1 = (bf16[16,24,2048]{2,1,0:T(8,128)(2,1)}, bf16[16,24,2048]{2,1,0:T(8,128)(2,1)}, bf16[2048,128]{1,0:T(8,128)(2,1)}) custom-call(bf16[14,24,2048]{2,1,0:T(8,128)(2,1)S(1)} %get-tuple-element.7.gate, bf16[14,24,2048]{2,1,0:T(8,128)(2,1)S(1)} %get-tuple-element.8.up, bf16[2048,128]{1,0:T(8,128)(2,1)S(1)} %get-tuple-element.9.router, ...), custom_call_target="tpu_custom_call" | custom-call | tf_op jit(solution)/shard_map/store/pallas_call | solution.py:313

commit v4 on v3

--- a/solution.py
+++ b/solution.py
@@ -18,7 +18,8 @@
 F32, BF16 = jnp.float32, jnp.bfloat16
 NEAR = [(dz, dx) for dz in (1, 7, 0) for dx in (2, 1, 3, 0) if dz or dx]
 FAR = [(dz, dx) for dz in (4, 3, 5, 2, 6) for dx in (2, 1, 3, 0)]
-MID = 1
+EARLY = 5
+MID = 2
 
 
 def merged(blocks, gate, up):
@@ -136,8 +137,10 @@
             pl.semaphore_wait(barrier, len(NEAR) + jnp.where(shard == 0, NE - 1, 0))
             tell(near_sem, 1)
 
-        for dz, dx in NEAR:
-            block_copy(p, dz, dx).start()
+        @pl.when(p < EARLY)
+        def _():
+            for dz, dx in NEAR:
+                block_copy(p, dz, dx).start()
 
         @pl.when(p == 0)
         def _():
@@ -170,6 +173,11 @@
     def _(p):
         for dz, dx in FAR:
             block_copy(p, dz, dx).start()
+
+        @pl.when(p >= EARLY)
+        def _():
+            for dz, dx in NEAR:
+                block_copy(p, dz, dx).start()
 
         @pl.when(p == 1)
         def _():

time: 81.7 us -> 81.4 us (level)
  no operation moved by 1% of the time
where the time goes in v4:
time: 81.4 us; the launch traced here: 80.5 us
  Pallas kernels  79.8 us (98%)
    pallas_call x1, Pallas kernels, shards(): pl.pallas_call(exchange, out_shape=(part, part, shapes[2], blocks), in_sp...  77.9 us
    pallas_call x1, Pallas kernels, shards(): pl.pallas_call(store, out_shape=shapes, in_specs=[vmem] * 4, out_specs=(h...  1.87 us

profile of v4, /device:TPU:6, one launch (start us, length us, event | category | flops | bytes accessed | tf_op | source)
XLA Modules:
  0.0 80.5 jit_solution(17108720965251208043)
XLA Ops:
  0.6 77.9 %exchange.1 = (bf16[14,24,2048]{2,1,0:T(8,128)(2,1)S(1)}, bf16[14,24,2048]{2,1,0:T(8,128)(2,1)S(1)}, bf16[2048,128]{1,0:T(8,128)(2,1)S(1)}, bf16[8,32,48,128]{3,2,1,0:T(8,128)(2,1)S(1)}) custom-call(f32[16,64,768]{2,1,0:T(8,128)} %mg.1, bf16[16,64,768]{2,1,0:T(8,128)(2,1)} %sg.1, f32[16,64,768]{2,1,0:T(8,128)} %mu.1, bf16[16,64,768]{2,1,0:T(8,128)(2,1)} %su.1, ...), custom_call_target="tpu_custom_call" | custom-call | tf_op jit(solution)/shard_map/exchange/pallas_call | solution.py:284
  78.6 1.9 %store.1 = (bf16[16,24,2048]{2,1,0:T(8,128)(2,1)}, bf16[16,24,2048]{2,1,0:T(8,128)(2,1)}, bf16[2048,128]{1,0:T(8,128)(2,1)}) custom-call(bf16[14,24,2048]{2,1,0:T(8,128)(2,1)S(1)} %get-tuple-element.7.gate, bf16[14,24,2048]{2,1,0:T(8,128)(2,1)S(1)} %get-tuple-element.8.up, bf16[2048,128]{1,0:T(8,128)(2,1)S(1)} %get-tuple-element.9.router, ...), custom_call_target="tpu_custom_call" | custom-call | tf_op jit(solution)/shard_map/store/pallas_call | solution.py:321

commit v5 on v4

--- a/solution.py
+++ b/solution.py
@@ -19,6 +19,7 @@
 NEAR = [(dz, dx) for dz in (1, 7, 0) for dx in (2, 1, 3, 0) if dz or dx]
 FAR = [(dz, dx) for dz in (4, 3, 5, 2, 6) for dx in (2, 1, 3, 0)]
 EARLY = 5
+SORTED = 5
 MID = 2
 
 
@@ -171,13 +172,25 @@
 
     @pl.loop(0, PAIRS)
     def _(p):
-        for dz, dx in FAR:
-            block_copy(p, dz, dx).start()
-
-        @pl.when(p >= EARLY)
+        @pl.when(p < SORTED)
+        def _():
+            for dz, dx in FAR:
+                block_copy(p, dz, dx).start()
+
+        @pl.when((p >= EARLY) & (p < SORTED))
         def _():
             for dz, dx in NEAR:
                 block_copy(p, dz, dx).start()
+
+        @pl.when(p >= SORTED)
+        def _():
+            for first in (True, False):
+                for dz in (4, 3, 5, 2, 6, 1, 7, 0):
+
+                    @pl.when((row[dz] < NX * 2) == first)
+                    def _():
+                        for dx in (2, 1, 3, 0) if dz else (2, 1, 3):
+                            block_copy(p, dz, dx).start()
 
         @pl.when(p == 1)
         def _():

time: 81.4 us -> 80.4 us (0.988)
  Pallas kernels: 79.8 us -> 78.8 us
    pallas_call x1, Pallas kernels: 77.9 us -> 76.9 us  [shards(): pl.pallas_call(exchange, out_shape=(part, part, shapes[2], blocks), in_sp...]
where the time goes in v5:
time: 80.4 us; the launch traced here: 79.4 us
  Pallas kernels  78.8 us (98%)
    pallas_call x1, Pallas kernels, shards(): pl.pallas_call(exchange, out_shape=(part, part, shapes[2], blocks), in_sp...  76.9 us
    pallas_call x1, Pallas kernels, shards(): pl.pallas_call(store, out_shape=shapes, in_specs=[vmem] * 4, out_specs=(h...  1.87 us

profile of v5, /device:TPU:6, one launch (start us, length us, event | category | flops | bytes accessed | tf_op | source)
XLA Modules:
  0.0 79.4 jit_solution(17654632478432858322)
XLA Ops:
  0.6 76.9 %exchange.1 = (bf16[14,24,2048]{2,1,0:T(8,128)(2,1)S(1)}, bf16[14,24,2048]{2,1,0:T(8,128)(2,1)S(1)}, bf16[2048,128]{1,0:T(8,128)(2,1)S(1)}, bf16[8,32,48,128]{3,2,1,0:T(8,128)(2,1)S(1)}) custom-call(f32[16,64,768]{2,1,0:T(8,128)} %mg.1, bf16[16,64,768]{2,1,0:T(8,128)(2,1)} %sg.1, f32[16,64,768]{2,1,0:T(8,128)} %mu.1, bf16[16,64,768]{2,1,0:T(8,128)(2,1)} %su.1, ...), custom_call_target="tpu_custom_call" | custom-call | tf_op jit(solution)/shard_map/exchange/pallas_call | solution.py:297
  77.6 1.9 %store.1 = (bf16[16,24,2048]{2,1,0:T(8,128)(2,1)}, bf16[16,24,2048]{2,1,0:T(8,128)(2,1)}, bf16[2048,128]{1,0:T(8,128)(2,1)}) custom-call(bf16[14,24,2048]{2,1,0:T(8,128)(2,1)S(1)} %get-tuple-element.7.gate, bf16[14,24,2048]{2,1,0:T(8,128)(2,1)S(1)} %get-tuple-element.8.up, bf16[2048,128]{1,0:T(8,128)(2,1)S(1)} %get-tuple-element.9.router, ...), custom_call_target="tpu_custom_call" | custom-call | tf_op jit(solution)/shard_map/store/pallas_call | solution.py:334

commit v6 on v5

--- a/solution.py
+++ b/solution.py
@@ -20,6 +20,7 @@
 FAR = [(dz, dx) for dz in (4, 3, 5, 2, 6) for dx in (2, 1, 3, 0)]
 EARLY = 5
 SORTED = 5
+TIERS = ((0, 2), (2, 3), (3, 8))
 MID = 2
 
 
@@ -184,10 +185,10 @@
 
         @pl.when(p >= SORTED)
         def _():
-            for first in (True, False):
+            for low, high in TIERS:
                 for dz in (4, 3, 5, 2, 6, 1, 7, 0):
 
-                    @pl.when((row[dz] < NX * 2) == first)
+                    @pl.when((row[dz] >= low * NX) & (row[dz] < high * NX))
                     def _():
                         for dx in (2, 1, 3, 0) if dz else (2, 1, 3):
                             block_copy(p, dz, dx).start()

time: 80.4 us -> 80.4 us (level)
  no operation moved by 1% of the time
where the time goes in v6:
time: 80.4 us; the launch traced here: 79.5 us
  Pallas kernels  78.8 us (98%)
    pallas_call x1, Pallas kernels, shards(): pl.pallas_call(exchange, out_shape=(part, part, shapes[2], blocks), in_sp...  76.9 us
    pallas_call x1, Pallas kernels, shards(): pl.pallas_call(store, out_shape=shapes, in_specs=[vmem] * 4, out_specs=(h...  1.87 us

profile of v6, /device:TPU:6, one launch (start us, length us, event | category | flops | bytes accessed | tf_op | source)
XLA Modules:
  0.0 79.5 jit_solution(15551952010020008615)
XLA Ops:
  0.6 76.9 %exchange.1 = (bf16[14,24,2048]{2,1,0:T(8,128)(2,1)S(1)}, bf16[14,24,2048]{2,1,0:T(8,128)(2,1)S(1)}, bf16[2048,128]{1,0:T(8,128)(2,1)S(1)}, bf16[8,32,48,128]{3,2,1,0:T(8,128)(2,1)S(1)}) custom-call(f32[16,64,768]{2,1,0:T(8,128)} %mg.1, bf16[16,64,768]{2,1,0:T(8,128)(2,1)} %sg.1, f32[16,64,768]{2,1,0:T(8,128)} %mu.1, bf16[16,64,768]{2,1,0:T(8,128)(2,1)} %su.1, ...), custom_call_target="tpu_custom_call" | custom-call | tf_op jit(solution)/shard_map/exchange/pallas_call | solution.py:298
  77.6 1.9 %store.1 = (bf16[16,24,2048]{2,1,0:T(8,128)(2,1)}, bf16[16,24,2048]{2,1,0:T(8,128)(2,1)}, bf16[2048,128]{1,0:T(8,128)(2,1)}) custom-call(bf16[14,24,2048]{2,1,0:T(8,128)(2,1)S(1)} %get-tuple-element.7.gate, bf16[14,24,2048]{2,1,0:T(8,128)(2,1)S(1)} %get-tuple-element.8.up, bf16[2048,128]{1,0:T(8,128)(2,1)S(1)} %get-tuple-element.9.router, ...), custom_call_target="tpu_custom_call" | custom-call | tf_op jit(solution)/shard_map/store/pallas_call | solution.py:335

commit v7 on v6

--- a/solution.py
+++ b/solution.py
@@ -20,7 +20,8 @@
 FAR = [(dz, dx) for dz in (4, 3, 5, 2, 6) for dx in (2, 1, 3, 0)]
 EARLY = 5
 SORTED = 5
-TIERS = ((0, 2), (2, 3), (3, 8))
+TOGETHER = 6
+TIERS = ((0, 2), (2, 8))
 MID = 2
 
 
@@ -183,15 +184,26 @@
             for dz, dx in NEAR:
                 block_copy(p, dz, dx).start()
 
-        @pl.when(p >= SORTED)
+        def send_tier(p, low, high):
+            for dz in (4, 3, 5, 2, 6, 1, 7, 0):
+
+                @pl.when((row[dz] >= low * NX) & (row[dz] < high * NX))
+                def _():
+                    for dx in (2, 1, 3, 0) if dz else (2, 1, 3):
+                        block_copy(p, dz, dx).start()
+
+        @pl.when((p >= SORTED) & (p < TOGETHER))
         def _():
             for low, high in TIERS:
-                for dz in (4, 3, 5, 2, 6, 1, 7, 0):
-
-                    @pl.when((row[dz] >= low * NX) & (row[dz] < high * NX))
-                    def _():
-                        for dx in (2, 1, 3, 0) if dz else (2, 1, 3):
-                            block_copy(p, dz, dx).start()
+                send_tier(p, low, high)
+
+        @pl.when(p == TOGETHER)
+        def _():
+            for low, high in TIERS:
+
+                @pl.loop(TOGETHER, PAIRS)
+                def _(q):
+                    send_tier(q, low, high)
 
         @pl.when(p == 1)
         def _():

time: 80.4 us -> 80.4 us (level)
  the two profiles are of different devices: /device:TPU:6 before, /device:TPU:72 now
where the time goes in v7:
time: 80.4 us; the launch traced here: 80.2 us
  Pallas kernels  79.6 us (99%)
    pallas_call x1, Pallas kernels, shards(): pl.pallas_call(exchange, out_shape=(part, part, shapes[2], blocks), in_sp...  77.7 us
    pallas_call x1, Pallas kernels, shards(): pl.pallas_call(store, out_shape=shapes, in_specs=[vmem] * 4, out_specs=(h...  1.87 us

profile of v7, /device:TPU:72, one launch (start us, length us, event | category | flops | bytes accessed | tf_op | source)
XLA Modules:
  0.0 80.2 jit_solution(8719305610498971916)
XLA Ops:
  0.6 77.7 %exchange.1 = (bf16[14,24,2048]{2,1,0:T(8,128)(2,1)S(1)}, bf16[14,24,2048]{2,1,0:T(8,128)(2,1)S(1)}, bf16[2048,128]{1,0:T(8,128)(2,1)S(1)}, bf16[8,32,48,128]{3,2,1,0:T(8,128)(2,1)S(1)}) custom-call(f32[16,64,768]{2,1,0:T(8,128)} %mg.1, bf16[16,64,768]{2,1,0:T(8,128)(2,1)} %sg.1, f32[16,64,768]{2,1,0:T(8,128)} %mu.1, bf16[16,64,768]{2,1,0:T(8,128)(2,1)} %su.1, ...), custom_call_target="tpu_custom_call" | custom-call | tf_op jit(solution)/shard_map/exchange/pallas_call | solution.py:310
  78.4 1.9 %store.1 = (bf16[16,24,2048]{2,1,0:T(8,128)(2,1)}, bf16[16,24,2048]{2,1,0:T(8,128)(2,1)}, bf16[2048,128]{1,0:T(8,128)(2,1)}) custom-call(bf16[14,24,2048]{2,1,0:T(8,128)(2,1)S(1)} %get-tuple-element.7.gate, bf16[14,24,2048]{2,1,0:T(8,128)(2,1)S(1)} %get-tuple-element.8.up, bf16[2048,128]{1,0:T(8,128)(2,1)S(1)} %get-tuple-element.9.router, ...), custom_call_target="tpu_custom_call" | custom-call | tf_op jit(solution)/shard_map/store/pallas_call | solution.py:347
